TPU v7x, 32 devices: a whole 2x2x4 slice. The times are simulated.
32 devices in a mesh: lat: 8 (over y, x, core), lon: 4 (over z).
Axes of the slice: x: 2, y: 2, z: 4, core: 2. Of those that a mesh axis runs over, the one named last changes fastest.
Arguments:
- coeffs_old: float32 [640, 2, 3, 50, 640], P(('lat', 'lon')), may hold values from -0.16 to 0.16
- noise: bfloat16 [640, 2, 3, 50, 640], P(('lat', 'lon')), may hold values from -6 to 6
- legendre: float32 [640, 640, 640], P(('lat', 'lon')), may hold values from -0.25 to 0.25
- decay: float32 [3], replicated, may hold values from 0.3 to 0.97
- amplitude: float32 [3, 640], replicated, may hold values from 0.005 to 0.05
- wavenumber_of_slot: int32 [640], replicated, may hold values from 0 to 639, as said below
- lat_order: int32 [640], replicated, may hold values from 0 to 639, each once
Outputs:
- coeffs_new: float32 [640, 2, 3, 50, 640], P(('lat', 'lon'))
- pattern: float32 [640, 50, 1280], P(('lat', 'lon'))
Inputs may be any that keep to these rules, and one draw needn't show every extreme that they name: `wavenumber_of_slot`: every wavenumber fills exactly one slot; the sums of the wavenumbers of one device's 20 slots differ between devices by less than 32. `lat_order`: every latitude stands in exactly one row.
All inputs are finite; a program needn't handle non-finite values.
Results may differ from a plain program's by a relative error of at most 0.0003.
Values sent between devices are 32-bit elements; how exact they have to be, the bound alone decides.
No kernel may reach another device: no remote copies, remote signals or barrier semaphores. Data moves between devices by JAX's collectives and lax.ppermute only.
A program may use at most 192 MiB of HBM per device.

v0:
```python
import jax
import jax.numpy as jnp
from jax import lax
from jax.experimental import pallas as pl
from jax.experimental.layout import Layout, with_layout_constraint
from jax.experimental.pallas import tpu as pltpu
from jax.sharding import PartitionSpec as P

TWO_PI = 6.283185307179586
LON = 1280
LANES = 128
AXES = ("lat", "lon")


def chunks_of(slots):
    if slots % 4:
        return (slots,)
    if slots >= 16:
        return (4, slots - 8, 4)
    return (slots,)


def round_up(value, unit):
    return -(-value // unit) * unit


def dense(values):
    slots, parts, scales, members, width = values.shape
    split = values.reshape(slots, parts, scales, members, width // LANES, LANES)
    split = with_layout_constraint(split, Layout((0, 2, 3, 4, 1, 5)))
    return split.transpose(0, 2, 3, 4, 1, 5).reshape(-1, LANES)


def undense(values, shape):
    slots, parts, scales, members, width = shape
    split = values.reshape(slots, scales, members, width // LANES, parts, LANES)
    return split.transpose(0, 1, 2, 4, 3, 5).reshape(slots, scales, members, parts, width).transpose(
        0, 3, 1, 2, 4
    )


def spectral_kernel(
    first, unit, count, groups, group_rows, members, rows_p, scales, width, base, waves, decay,
    old, noise, legendre, amplitude, select, *rest
):
    new, out, drive, loud, spectrum, rows = rest[0 if first else 1 :]
    step = pl.program_id(0)
    half = spectrum.shape[1] // 4
    blocks = count * groups
    tiles = width // LANES
    stride = 2 * tiles
    per_slot = scales * members * stride

    @pl.when(step == 0)
    def _():
        spectrum[...] = jnp.zeros_like(spectrum)
        if rows_p != 2 * unit * pl.num_programs(0):
            out[...] = jnp.zeros_like(out)
        for k in range(scales):
            d = jnp.full((1, LANES), decay[k], jnp.float32)
            factor = jnp.sqrt(1.0 - d * d)[:, :1]
            drive[k : k + 1] = amplitude[k : k + 1] * factor

    loud[...] = noise[...].astype(jnp.float32)
    lane = lax.broadcasted_iota(jnp.int32, (1, LANES), 1)
    wide_lane = lax.broadcasted_iota(jnp.int32, (blocks, LANES), 1)
    nt = (((1,), (1,)), ((), ()))
    for u in range(unit):
        wave = waves[base[0] + step * unit + u]
        gains = pltpu.roll(drive[...], lax.rem(width - wave, width), 1)
        for tile in range(tiles):
            live = lane + (tile * LANES) + wave < width
            keep = [jnp.where(live, decay[k], 0.0) for k in range(scales)]
            gain = [
                jnp.where(live, gains[k : k + 1, tile * LANES : (tile + 1) * LANES], 0.0)
                for k in range(scales)
            ]
            for r in range(2):
                total = None
                for k in range(scales):
                    at = pl.ds(u * per_slot + k * members * stride + 2 * tile + r, members, stride=stride)
                    fresh = keep[k] * old[at, :] + gain[k] * loud[at, :]
                    new[at, :] = fresh
                    total = fresh if total is None else total + fresh
                high = total.astype(jnp.bfloat16)
                low = (total - high.astype(jnp.float32)).astype(jnp.bfloat16)
                cut = slice(tile * LANES, (tile + 1) * LANES)
                spectrum[u, r * half : r * half + members, cut] = high
                spectrum[u, (2 + r) * half : (2 + r) * half + members, cut] = low
        basis = legendre[u]
        basis_high = basis.astype(jnp.bfloat16)
        basis_low = (basis - basis_high.astype(jnp.float32)).astype(jnp.bfloat16)
        wide = lax.dot_general(basis_high, spectrum[u], nt, preferred_element_type=jnp.float32)
        narrow = lax.dot_general(
            basis_low, spectrum[u, : 2 * half], nt, preferred_element_type=jnp.float32
        )
        field = wide[:, : 2 * half] + wide[:, 2 * half :] + narrow
        field_high = field.astype(jnp.bfloat16)
        field_low = (field - field_high.astype(jnp.float32)).astype(jnp.bfloat16)
        both = jnp.dot(
            select[...],
            jnp.concatenate([field_high, field_low], axis=1),
            preferred_element_type=jnp.float32,
        )
        rows[u] = both[:, : 2 * half] + both[:, 2 * half :]
        for r in range(2):
            packed = [None, None]
            for i in range(group_rows):
                start = i * members
                piece = rows[u, pl.ds(i, blocks, stride=group_rows), :]
                shift = (start - r * half) % LANES
                if shift:
                    piece = pltpu.roll(piece, shift, 1)
                for tile in range(2):
                    begin = max(start - tile * LANES, 0)
                    end = min(start + members - tile * LANES, LANES)
                    if begin >= end:
                        continue
                    if packed[tile] is None:
                        packed[tile] = piece
                    else:
                        packed[tile] = jnp.where(wide_lane < begin, packed[tile], piece)
            for tile in range(2):
                at = pl.ds(tile * rows_p + 2 * (step * unit + u) + r, blocks, stride=2 * rows_p)
                out[at, :] = packed[tile]


def spectral(old, noise, legendre, amplitude, decay, waves, base, select, shape, start, slots, previous, count, groups, group_rows):
    _, _, scales, members, width = shape
    unit = 2 if slots % 2 == 0 else slots
    rows_p = round_up(2 * slots, 8)
    first = previous is None
    size = groups * 2 * rows_p
    block = unit * scales * members * 2 * (width // LANES)
    skip = start // unit

    def body(*refs):
        spectral_kernel(
            first, unit, count, groups, group_rows, members, rows_p, scales, width, *refs
        )

    state = pl.BlockSpec((block, LANES), lambda i: (skip + i, 0))
    in_specs = [
        pl.BlockSpec(memory_space=pltpu.SMEM),
        pl.BlockSpec(memory_space=pltpu.SMEM),
        pl.BlockSpec(memory_space=pltpu.SMEM),
        state,
        state,
        pl.BlockSpec((unit,) + legendre.shape[1:], lambda i: (skip + i, 0, 0)),
        pl.BlockSpec(amplitude.shape, lambda i: (0, 0)),
        pl.BlockSpec(select.shape, lambda i: (0, 0)),
    ]
    args = [base + start, waves, decay, old, noise, legendre, amplitude, select]
    aliases = {}
    if not first:
        in_specs.append(pl.BlockSpec(memory_space=pl.ANY))
        aliases = {len(args): 0}
        args.append(previous)
    new, messages = pl.pallas_call(
        body,
        grid=(slots // unit,),
        in_specs=in_specs,
        out_specs=[state, pl.BlockSpec((count * size, LANES), lambda i: (0, 0))],
        out_shape=[
            jax.ShapeDtypeStruct(old.shape, jnp.float32),
            jax.ShapeDtypeStruct((count * size, LANES), jnp.float32),
        ],
        scratch_shapes=[
            pltpu.VMEM((8, width), jnp.float32),
            pltpu.VMEM((block, LANES), jnp.float32),
            pltpu.VMEM((unit, 4 * 64, width), jnp.bfloat16),
            pltpu.VMEM((unit, legendre.shape[1], LANES), jnp.float32),
        ],
        input_output_aliases=aliases,
        compiler_params=pltpu.CompilerParams(dimension_semantics=("arbitrary",)),
        cost_estimate=pl.CostEstimate(
            flops=slots * 2 * 10**9 // 4, bytes_accessed=slots * 3500000, transcendentals=0
        ),
        name="spectral",
    )(*args)
    return new, messages.reshape(count, size, LANES)


def synthesis_kernel(has_previous, final, count, rows_p, members, group_rows, fine, coarse, sources, *rest):
    previous = None
    if has_previous:
        previous = rest[0]
        rest = rest[1:]
    out, table_high, table_low, stack = rest
    group = pl.program_id(0)
    length = table_high.shape[1]

    @pl.when(group == 0)
    def _():
        even = fine[0]
        odd = fine[1]
        for b in range(length // LANES):
            values = even * coarse[0, :, b : b + 1] - odd * coarse[1, :, b : b + 1]
            high = values.astype(jnp.bfloat16)
            cut = slice(b * LANES, (b + 1) * LANES)
            table_high[:, cut] = high
            table_low[:, cut] = (values - high.astype(jnp.float32)).astype(jnp.bfloat16)

    for d in range(count):
        for tile in range(2):
            offset = pl.multiple_of((group * 2 + tile) * rows_p, 8)
            stack[d * rows_p : (d + 1) * rows_p, tile * LANES : (tile + 1) * LANES] = sources[
                d, pl.ds(offset, rows_p), :
            ]
    turned = stack[...].T
    high = turned.astype(jnp.bfloat16)
    low = (turned - high.astype(jnp.float32)).astype(jnp.bfloat16)
    result = jnp.dot(high, table_high[...], preferred_element_type=jnp.float32)
    result += jnp.dot(low, table_high[...], preferred_element_type=jnp.float32)
    result += jnp.dot(high, table_low[...], preferred_element_type=jnp.float32)
    if has_previous:
        result += previous[0]
    if final:
        for i in range(group_rows):
            out[i] = result[i * members : (i + 1) * members]
    else:
        out[0] = result


def synthesis(fine, coarse, sources, previous, final, groups, group_rows, members, length):
    count = sources.shape[0]
    depth = fine.shape[1]
    rows_p = depth // count

    def body(*refs):
        synthesis_kernel(previous is not None, final, count, rows_p, members, group_rows, *refs)

    in_specs = [
        pl.BlockSpec(fine.shape, lambda g: (0, 0, 0)),
        pl.BlockSpec(coarse.shape, lambda g: (0, 0, 0)),
        pl.BlockSpec(sources.shape, lambda g: (0, 0, 0)),
    ]
    args = [fine, coarse, sources]
    partial = pl.BlockSpec((1, 2 * LANES, length), lambda g: (g, 0, 0))
    aliases = {}
    if previous is not None:
        in_specs.append(partial)
        if not final:
            aliases = {len(args): 0}
        args.append(previous)
    if final:
        out_spec = pl.BlockSpec((group_rows, members, length), lambda g: (g, 0, 0))
        out_shape = jax.ShapeDtypeStruct((groups * group_rows, members, length), jnp.float32)
    else:
        out_spec = partial
        out_shape = jax.ShapeDtypeStruct((groups, 2 * LANES, length), jnp.float32)
    return pl.pallas_call(
        body,
        grid=(groups,),
        in_specs=in_specs,
        out_specs=out_spec,
        out_shape=out_shape,
        scratch_shapes=[
            pltpu.VMEM((depth, length), jnp.bfloat16),
            pltpu.VMEM((depth, length), jnp.bfloat16),
            pltpu.VMEM((depth, 2 * LANES), jnp.float32),
        ],
        input_output_aliases=aliases,
        compiler_params=pltpu.CompilerParams(dimension_semantics=("arbitrary",)),
        cost_estimate=pl.CostEstimate(
            flops=6 * groups * 256 * depth * length, bytes_accessed=12 * 10**6, transcendentals=0
        ),
        name="synthesis",
    )(*args)


def synthesis_tables(waves, parts, length):
    count, slots = waves.shape
    numbers = []
    start = 0
    for size in parts:
        rows = jnp.repeat(waves[:, start : start + size], 2, axis=1)
        pad = round_up(2 * size, 8) - 2 * size
        numbers.append(jnp.pad(rows, ((0, 0), (0, pad)), constant_values=-1).reshape(-1))
        start += size
    number = jnp.concatenate(numbers)[:, None]
    lane = lax.broadcasted_iota(jnp.int32, (number.shape[0], LANES), 1)
    part = lax.broadcasted_iota(jnp.int32, (number.shape[0], LANES), 0) % 2
    weight = jnp.where(number == 0, 1.0, jnp.where(number < 0, 0.0, 2.0)).astype(jnp.float32)
    wave = jnp.maximum(number, 0)
    near = ((wave * lane + part * (length // 4)) % length).astype(jnp.float32) * (TWO_PI / length)
    far = ((wave * (lane * LANES % length)) % length).astype(jnp.float32) * (TWO_PI / length)
    fine = jnp.stack([weight * jnp.cos(near), weight * jnp.sin(near)])
    coarse = jnp.stack([jnp.cos(far), jnp.sin(far)])
    return fine, coarse


def local(coeffs_old, noise, legendre, decay, amplitude, wavenumber_of_slot, lat_order):
    lat_count = lax.axis_size("lat")
    lon_count = lax.axis_size("lon")
    count = lat_count * lon_count
    me = lax.axis_index("lat") * lon_count + lax.axis_index("lon")
    shape = coeffs_old.shape
    slots, _, scales, members, width = shape
    latitudes = lat_order.shape[0]
    rows = latitudes // count
    group_rows = (2 * LANES) // members
    while rows % group_rows:
        group_rows -= 1
    groups = rows // group_rows

    column = lax.broadcasted_iota(jnp.int32, (latitudes, latitudes), 1)
    select = (lat_order[:, None] == column).astype(jnp.bfloat16)
    base = (me * slots).reshape(1).astype(jnp.int32)

    old = dense(coeffs_old)
    fresh_noise = dense(noise)
    parts = chunks_of(slots)
    new = None
    received = []
    start = 0
    waves = wavenumber_of_slot
    for size in parts:
        new, messages = spectral(
            old, fresh_noise, legendre, amplitude, decay, wavenumber_of_slot, base, select, shape,
            start, size, new, count, groups, group_rows,
        )
        if start == 0:
            messages, waves = lax.optimization_barrier((messages, waves))
        received.append(lax.all_to_all(messages, AXES, 0, 0, tiled=True))
        start += size
    fine, coarse = synthesis_tables(waves.reshape(count, slots), parts, LON)
    pattern = None
    start = 0
    for index, size in enumerate(parts):
        depth = count * round_up(2 * size, 8)
        pattern = synthesis(
            fine[:, start : start + depth], coarse[:, start : start + depth], received[index],
            pattern, index == len(parts) - 1, groups, group_rows, members, LON,
        )
        start += depth
    return (undense(new, shape), pattern)


def solution(mesh):
    in_specs = (
        P(AXES, None, None, None, None),
        P(AXES, None, None, None, None),
        P(AXES, None, None),
        P(),
        P(),
        P(),
        P(),
    )
    out_specs = (P(AXES, None, None, None, None), P(AXES, None, None))
    return jax.shard_map(local, mesh=mesh, in_specs=in_specs, out_specs=out_specs, check_vma=False)
```

profile of v0, /device:TPU:0, one launch (start us, length us, event | category | flops | bytes accessed | tf_op | source)
XLA Modules:
  0.0 163.6 jit_solution(7351111091420219134)
XLA Ops:
  0.6 1.8 %fusion.refs_7_ = bf16[640,640]{1,0:T(8,128)(2,1)} fusion(s32[640]{0:T(1024)} %param.13), kind=kLoop, calls=%fused_computation.1 | loop fusion | flops 819200 | bytes 821760 | tf_op jit(solution)/shard_map/convert_element_type | solution.py:308
  2.5 9.6 %spectral.3 = (f32[30000,128]{1,0:T(8,128)}, f32[2048,128]{1,0:T(8,128)}) custom-call(s32[1]{0:T(128)} %bitcast.refs_0_, s32[640]{0:T(1024)} %refs_1_.5, f32[3]{0:T(128)} %refs_2_.5, f32[30000,128]{1,0:T(8,128)} %bitcast.21, bf16[30000,128]{1,0:T(8,128)(2,1)} %bitcast.24, f32[20,640,640]{2,1,0:T(8,128)} %refs_5_.5, f32[3,640]{1,0:T(4,128)} %refs_6_.5, ...), custom_call_target="tpu_custom_call" | custom-call | flops 2000000000 | bytes 14000000 | tf_op jit(solution)/shard_map/spectral/pallas_call | solution.py:159
  12.0 7.3 %all-to-all-start.2 = ((f32[32,64,128]{2,1,0:T(8,128)}), f32[32,64,128]{2,1,0:T(8,128)S(1)}, u32[]{:S(2)}, u32[]{:S(2)}) async-start(f32[32,64,128]{2,1,0:T(8,128)} %bitcast.30), calls=%async_computation.2 | async-start | bytes 2097152 | tf_op jit(solution)/shard_map/all_to_all | solution.py:325
  19.4 21.3 %spectral.4 = (f32[30000,128]{1,0:T(8,128)}, f32[6144,128]{1,0:T(8,128)}) custom-call(s32[1]{0:T(128)S(6)} %add.67.refs_0_, s32[640]{0:T(1024)} %refs_1_.5, f32[3]{0:T(128)} %refs_2_.5, f32[30000,128]{1,0:T(8,128)} %bitcast.22, bf16[30000,128]{1,0:T(8,128)(2,1)} %bitcast.25, f32[20,640,640]{2,1,0:T(8,128)} %refs_5_.5, ...), custom_call_target="tpu_custom_call", output_to_operand_aliasing={{0}: (8, {})} | custom-call | flops 6000000000 | bytes 42000000 | tf_op jit(solution)/shard_map/spectral/pallas_call | solution.py:159
  40.6 0.0 copy-start.3
  40.7 3.6 %all-to-all-done.2.refs_2_ = f32[32,64,128]{2,1,0:T(8,128)S(1)} async-done(((f32[32,64,128]{2,1,0:T(8,128)}), f32[32,64,128]{2,1,0:T(8,128)S(1)}, u32[]{:S(2)}, u32[]{:S(2)}) %all-to-all-start.2) | async-done | bytes 1048608 | tf_op jit(solution)/shard_map/all_to_all | solution.py:325
  44.3 0.0 copy-start.2
  44.3 1.0 copy-done.2
  45.3 4.6 %all-to-all-start.1 = ((f32[32,192,128]{2,1,0:T(8,128)}), f32[32,192,128]{2,1,0:T(8,128)S(1)}, u32[]{:S(2)}, u32[]{:S(2)}) async-start(f32[32,192,128]{2,1,0:T(8,128)} %bitcast.28), calls=%async_computation.1 | async-start | bytes 6291456 | tf_op jit(solution)/shard_map/all_to_all | solution.py:325
  49.8 0.0 copy-done.3
  49.9 0.1 reshape.574
  50.0 0.1 slice.37
  50.0 0.1 fusion.19
  50.1 0.1 broadcast_in_dim.23
  50.2 0.2 concatenate.20
  50.4 0.1 broadcast_in_dim.24
  50.5 0.1 concatenate.21
  50.6 0.1 broadcast_in_dim.25
  50.7 0.2 concatenate.22
  51.0 9.6 %spectral.5 = (f32[30000,128]{1,0:T(8,128)}, f32[2048,128]{1,0:T(8,128)}) custom-call(s32[1]{0:T(128)S(6)} %add.66.refs_0_, s32[640]{0:T(1024)} %refs_1_.5, f32[3]{0:T(128)} %refs_2_.5, f32[30000,128]{1,0:T(8,128)} %bitcast.23, bf16[30000,128]{1,0:T(8,128)(2,1)} %bitcast.26, f32[20,640,640]{2,1,0:T(8,128)} %refs_5_.5, ...), custom_call_target="tpu_custom_call", output_to_operand_aliasing={{0}: (8, {})} | custom-call | flops 2000000000 | bytes 14000000 | tf_op jit(solution)/shard_map/spectral/pallas_call | solution.py:159
  60.6 59.2 %all-to-all-done.1.refs_2_ = f32[32,192,128]{2,1,0:T(8,128)S(1)} async-done(((f32[32,192,128]{2,1,0:T(8,128)}), f32[32,192,128]{2,1,0:T(8,128)S(1)}, u32[]{:S(2)}, u32[]{:S(2)}) %all-to-all-start.1) | async-done | bytes 3145760 | tf_op jit(solution)/shard_map/all_to_all | solution.py:325
  119.8 0.0 copy-start.1
  119.8 1.7 %copy-done.1 = f32[32,192,128]{2,1,0:T(8,128)} copy-done((f32[32,192,128]{2,1,0:T(8,128)}, f32[32,192,128]{2,1,0:T(8,128)S(1)}, u32[]{:S(2)}) %copy-start.1) | copy-done | bytes 3145752
  121.5 5.0 %all-to-all-start = ((f32[32,64,128]{2,1,0:T(8,128)}), f32[32,64,128]{2,1,0:T(8,128)S(1)}, u32[]{:S(2)}, u32[]{:S(2)}) async-start(f32[32,64,128]{2,1,0:T(8,128)} %bitcast.29), calls=%async_computation | async-start | bytes 2097152 | tf_op jit(solution)/shard_map/all_to_all | solution.py:325
  126.5 5.7 %fusion.10 = (f32[1,1280,128]{2,1,0:T(8,128)S(1)}, f32[1,1280,128]{2,1,0:T(8,128)S(1)}, f32[1,1280,128]{2,1,0:T(8,128)S(1)}, f32[1,1280,128]{2,1,0:T(8,128)S(1)}) fusion(s32[128]{0:T(128)S(1)} %multiply_remainder_fusion.1, s32[128]{0:T(128)S(1)} %broadcast_add_fusion, s32[1280]{0:T(1024)S(1)} %broadcast_maximum_fusion, ...), kind=kLoop, calls=%fused_computation.18 | loop fusion | flops 3932160 | bytes 2644352 | tf_op jit(solution)/shard_map/cos | solution.py:289
  132.3 1.0 pad_maximum_fusion
  133.3 1.4 fusion.1
  134.6 6.5 %synthesis.3.refs_3_ = f32[4,256,1280]{2,1,0:T(8,128)} custom-call(f32[2,256,128]{2,1,0:T(8,128)} %get-tuple-element.33.refs_0_, f32[2,256,128]{2,1,0:T(8,128)} %get-tuple-element.18.refs_1_, f32[32,64,128]{2,1,0:T(8,128)} %copy-done.2), custom_call_target="tpu_custom_call" | custom-call | flops 2013265920 | bytes 12000000 | tf_op jit(solution)/shard_map/synthesis/pallas_call | solution.py:252
  141.2 13.4 %synthesis.4.refs_3_ = f32[4,256,1280]{2,1,0:T(8,128)} custom-call(f32[2,768,128]{2,1,0:T(8,128)} %get-tuple-element.31.refs_0_, f32[2,768,128]{2,1,0:T(8,128)} %get-tuple-element.30.refs_1_, f32[32,192,128]{2,1,0:T(8,128)} %copy-done.1, f32[4,256,1280]{2,1,0:T(8,128)} %synthesis.3.refs_3_), custom_call_target="tpu_custom_call", output_to_operand_aliasing={{}: (3, {})} | custom-call | flops 6039797760 | bytes 12000000 | tf_op jit(solution)/shard_map/synthesis/pallas_call | solution.py:252
  154.5 0.0 all-to-all-done.refs_2_
  154.5 0.0 copy-start
  154.5 1.0 copy-done
  155.5 8.1 %synthesis.5 = f32[20,50,1280]{2,1,0:T(8,128)} custom-call(f32[2,256,128]{2,1,0:T(8,128)} %get-tuple-element.32.refs_0_, f32[2,256,128]{2,1,0:T(8,128)} %get-tuple-element.19.refs_1_, f32[32,64,128]{2,1,0:T(8,128)} %copy-done, f32[4,256,1280]{2,1,0:T(8,128)} %synthesis.4.refs_3_), custom_call_target="tpu_custom_call" | custom-call | flops 2013265920 | bytes 12000000 | tf_op jit(solution)/shard_map/synthesis/pallas_call | solution.py:252
  (12 shorter events, 0.1 us)
Async XLA Ops:
  12.0 32.3 %all-to-all-start.2 = ((f32[32,64,128]{2,1,0:T(8,128)}), f32[32,64,128]{2,1,0:T(8,128)S(1)}, u32[]{:S(2)}, u32[]{:S(2)}) async-start(f32[32,64,128]{2,1,0:T(8,128)} %bitcast.30), calls=%async_computation.2 | async-start | bytes 2097152 | tf_op jit(solution)/shard_map/all_to_all | solution.py:325
  40.6 9.2 %copy-start.3 = (s32[640]{0:T(1024)S(1)}, s32[640]{0:T(1024)}, u32[]{:S(2)}) copy-start(s32[640]{0:T(1024)} %refs_1_.5) | copy-start | bytes 7684
  44.3 1.0 copy-start.2
  45.3 74.5 %all-to-all-start.1 = ((f32[32,192,128]{2,1,0:T(8,128)}), f32[32,192,128]{2,1,0:T(8,128)S(1)}, u32[]{:S(2)}, u32[]{:S(2)}) async-start(f32[32,192,128]{2,1,0:T(8,128)} %bitcast.28), calls=%async_computation.1 | async-start | bytes 6291456 | tf_op jit(solution)/shard_map/all_to_all | solution.py:325
  119.8 1.7 %copy-start.1 = (f32[32,192,128]{2,1,0:T(8,128)}, f32[32,192,128]{2,1,0:T(8,128)S(1)}, u32[]{:S(2)}) copy-start(f32[32,192,128]{2,1,0:T(8,128)S(1)} %all-to-all-done.1.refs_2_) | copy-start | bytes 9437188
  121.5 33.1 %all-to-all-start = ((f32[32,64,128]{2,1,0:T(8,128)}), f32[32,64,128]{2,1,0:T(8,128)S(1)}, u32[]{:S(2)}, u32[]{:S(2)}) async-start(f32[32,64,128]{2,1,0:T(8,128)} %bitcast.29), calls=%async_computation | async-start | bytes 2097152 | tf_op jit(solution)/shard_map/all_to_all | solution.py:325
  154.5 1.0 copy-start
where the time goes:
time: 164 us
  Pallas kernels  68.4 us (42%)
  waiting for transfers between devices  62.8 us (38%)
  starting transfers between devices  16.9 us (10%)
  other arithmetic  9.99 us (6%)
  local copies, waits for them, and re-layouts  4.68 us (3%)
    all_to_all x3, waiting for transfers between devices, local(): received.append(lax.all_to_all(messages, AXES, 0, 0, tiled=True))  62.8 us
    pallas_call x3, Pallas kernels, spectral(): pl.pallas_call(body, grid=(slots // unit,), in_specs=in_specs, out_specs=...  40.4 us
    pallas_call x3, Pallas kernels, synthesis(): pl.pallas_call(body, grid=(groups,), in_specs=in_specs, out_specs=out_spe...  27.9 us
    all_to_all x3, starting transfers between devices, local(): received.append(lax.all_to_all(messages, AXES, 0, 0, tiled=True))  16.9 us
    cos x1, other arithmetic, synthesis_tables(): coarse = jnp.stack([jnp.cos(far), jnp.sin(far)])  5.72 us
    unnamed x10, local copies, waits for them, and re-layouts  3.69 us
  transfers between devices with their start and end apart: 3, of which 2 were waited for; matrix products, arithmetic and copies ran while one was open for 6% of the time, Pallas kernels for 31%

commit v1 on v0

--- a/solution.py
+++ b/solution.py
@@ -40,10 +40,10 @@
 
 
 def spectral_kernel(
-    first, unit, count, groups, group_rows, members, rows_p, scales, width, base, waves, decay,
-    old, noise, legendre, amplitude, select, *rest
+    first, slots, unit, count, groups, group_rows, members, rows_p, scales, width, base, waves,
+    decay, old, noise, legendre, amplitude, order, *rest
 ):
-    new, out, drive, loud, spectrum, rows = rest[0 if first else 1 :]
+    new, out, drive, loud, spectrum, rows, select = rest[0 if first else 1 :]
     step = pl.program_id(0)
     half = spectrum.shape[1] // 4
     blocks = count * groups
@@ -54,12 +54,20 @@
     @pl.when(step == 0)
     def _():
         spectrum[...] = jnp.zeros_like(spectrum)
-        if rows_p != 2 * unit * pl.num_programs(0):
+        if rows_p != 2 * slots:
             out[...] = jnp.zeros_like(out)
         for k in range(scales):
             d = jnp.full((1, LANES), decay[k], jnp.float32)
             factor = jnp.sqrt(1.0 - d * d)[:, :1]
             drive[k : k + 1] = amplitude[k : k + 1] * factor
+        lines = order.shape[0]
+        listed = order[...].astype(jnp.float32)
+        padding = jnp.zeros((round_up(lines, 8) - lines, LANES), jnp.float32)
+        listed = jnp.concatenate([listed, padding], axis=0).T
+        latitude = lax.broadcasted_iota(jnp.int32, (LANES, select.shape[1]), 1).astype(jnp.float32)
+        for b in range(lines):
+            hit = jnp.where(listed[:, b : b + 1] == latitude, 1.0, 0.0)
+            select[b * LANES : (b + 1) * LANES] = hit.astype(jnp.bfloat16)
 
     loud[...] = noise[...].astype(jnp.float32)
     lane = lax.broadcasted_iota(jnp.int32, (1, LANES), 1)
@@ -125,7 +133,7 @@
                 out[at, :] = packed[tile]
 
 
-def spectral(old, noise, legendre, amplitude, decay, waves, base, select, shape, start, slots, previous, count, groups, group_rows):
+def spectral(old, noise, legendre, amplitude, decay, waves, base, order, shape, start, slots, previous, count, groups, group_rows):
     _, _, scales, members, width = shape
     unit = 2 if slots % 2 == 0 else slots
     rows_p = round_up(2 * slots, 8)
@@ -136,7 +144,7 @@
 
     def body(*refs):
         spectral_kernel(
-            first, unit, count, groups, group_rows, members, rows_p, scales, width, *refs
+            first, slots, unit, count, groups, group_rows, members, rows_p, scales, width, *refs
         )
 
     state = pl.BlockSpec((block, LANES), lambda i: (skip + i, 0))
@@ -148,9 +156,9 @@
         state,
         pl.BlockSpec((unit,) + legendre.shape[1:], lambda i: (skip + i, 0, 0)),
         pl.BlockSpec(amplitude.shape, lambda i: (0, 0)),
-        pl.BlockSpec(select.shape, lambda i: (0, 0)),
+        pl.BlockSpec(order.shape, lambda i: (0, 0)),
     ]
-    args = [base + start, waves, decay, old, noise, legendre, amplitude, select]
+    args = [base + start, waves, decay, old, noise, legendre, amplitude, order]
     aliases = {}
     if not first:
         in_specs.append(pl.BlockSpec(memory_space=pl.ANY))
@@ -170,9 +178,12 @@
             pltpu.VMEM((block, LANES), jnp.float32),
             pltpu.VMEM((unit, 4 * 64, width), jnp.bfloat16),
             pltpu.VMEM((unit, legendre.shape[1], LANES), jnp.float32),
+            pltpu.VMEM((legendre.shape[1], legendre.shape[1]), jnp.bfloat16),
         ],
         input_output_aliases=aliases,
-        compiler_params=pltpu.CompilerParams(dimension_semantics=("arbitrary",)),
+        compiler_params=pltpu.CompilerParams(
+            dimension_semantics=("arbitrary",), vmem_limit_bytes=65400 * 2**10
+        ),
         cost_estimate=pl.CostEstimate(
             flops=slots * 2 * 10**9 // 4, bytes_accessed=slots * 3500000, transcendentals=0
         ),
@@ -181,87 +192,96 @@
     return new, messages.reshape(count, size, LANES)
 
 
-def synthesis_kernel(has_previous, final, count, rows_p, members, group_rows, fine, coarse, sources, *rest):
+def table_kernel(fine, coarse, high, low):
+    even = fine[0]
+    odd = fine[1]
+    for b in range(high.shape[1] // LANES):
+        values = even * coarse[0, :, b : b + 1] - odd * coarse[1, :, b : b + 1]
+        rounded = values.astype(jnp.bfloat16)
+        cut = slice(b * LANES, (b + 1) * LANES)
+        high[:, cut] = rounded
+        low[:, cut] = (values - rounded.astype(jnp.float32)).astype(jnp.bfloat16)
+
+
+def expand_tables(fine, coarse, start, depth, length):
+    rows = 256 if start % 256 == 0 and depth % 256 == 0 else depth
+    factor = pl.BlockSpec((2, rows, LANES), lambda i: (0, start // rows + i, 0))
+    table = pl.BlockSpec((rows, length), lambda i: (i, 0))
+    return pl.pallas_call(
+        table_kernel,
+        grid=(depth // rows,),
+        in_specs=[factor, factor],
+        out_specs=[table, table],
+        out_shape=[jax.ShapeDtypeStruct((depth, length), jnp.bfloat16)] * 2,
+        compiler_params=pltpu.CompilerParams(
+            dimension_semantics=("arbitrary",), vmem_limit_bytes=16 * 2**20
+        ),
+        cost_estimate=pl.CostEstimate(
+            flops=2 * 10**9 * depth // 1024, bytes_accessed=depth * length * 4, transcendentals=0
+        ),
+        name="tables",
+    )(fine, coarse)
+
+
+def synthesis_kernel(has_previous, final, groups, group_rows, members, table_high, table_low, sources, *rest):
     previous = None
     if has_previous:
         previous = rest[0]
         rest = rest[1:]
-    out, table_high, table_low, stack = rest
-    group = pl.program_id(0)
-    length = table_high.shape[1]
-
-    @pl.when(group == 0)
-    def _():
-        even = fine[0]
-        odd = fine[1]
-        for b in range(length // LANES):
-            values = even * coarse[0, :, b : b + 1] - odd * coarse[1, :, b : b + 1]
-            high = values.astype(jnp.bfloat16)
-            cut = slice(b * LANES, (b + 1) * LANES)
-            table_high[:, cut] = high
-            table_low[:, cut] = (values - high.astype(jnp.float32)).astype(jnp.bfloat16)
-
-    for d in range(count):
-        for tile in range(2):
-            offset = pl.multiple_of((group * 2 + tile) * rows_p, 8)
-            stack[d * rows_p : (d + 1) * rows_p, tile * LANES : (tile + 1) * LANES] = sources[
-                d, pl.ds(offset, rows_p), :
-            ]
-    turned = stack[...].T
-    high = turned.astype(jnp.bfloat16)
-    low = (turned - high.astype(jnp.float32)).astype(jnp.bfloat16)
+    (out,) = rest
+    count = sources.shape[0]
+    depth = table_high.shape[0]
+    rows_p = depth // count
+
+    pieces = []
+    for tile in range(2):
+        pieces.append(sources[:, tile * rows_p : (tile + 1) * rows_p, :].reshape(depth, LANES).T)
+    piece = jnp.concatenate(pieces, axis=0)
+    high = piece.astype(jnp.bfloat16)
+    low = (piece - high.astype(jnp.float32)).astype(jnp.bfloat16)
     result = jnp.dot(high, table_high[...], preferred_element_type=jnp.float32)
     result += jnp.dot(low, table_high[...], preferred_element_type=jnp.float32)
     result += jnp.dot(high, table_low[...], preferred_element_type=jnp.float32)
     if has_previous:
-        result += previous[0]
+        result += previous[...]
     if final:
         for i in range(group_rows):
             out[i] = result[i * members : (i + 1) * members]
     else:
-        out[0] = result
-
-
-def synthesis(fine, coarse, sources, previous, final, groups, group_rows, members, length):
-    count = sources.shape[0]
-    depth = fine.shape[1]
-    rows_p = depth // count
+        out[...] = result
+
+
+def synthesis(tables, sources, previous, final, groups, group_rows, members):
+    depth, length = tables[0].shape
 
     def body(*refs):
-        synthesis_kernel(previous is not None, final, count, rows_p, members, group_rows, *refs)
-
-    in_specs = [
-        pl.BlockSpec(fine.shape, lambda g: (0, 0, 0)),
-        pl.BlockSpec(coarse.shape, lambda g: (0, 0, 0)),
-        pl.BlockSpec(sources.shape, lambda g: (0, 0, 0)),
-    ]
-    args = [fine, coarse, sources]
-    partial = pl.BlockSpec((1, 2 * LANES, length), lambda g: (g, 0, 0))
-    aliases = {}
+        synthesis_kernel(previous is not None, final, groups, group_rows, members, *refs)
+
+    rows_p = depth // sources.shape[0]
+    table = pl.BlockSpec((depth, length), lambda b: (0, 0))
+    partial = pl.BlockSpec((2 * LANES, length), lambda b: (b, 0))
+    in_specs = [table, table, pl.BlockSpec((sources.shape[0], 2 * rows_p, LANES), lambda b: (0, b, 0))]
+    space = pltpu.VMEM if final else pltpu.HBM
+    args = [pltpu.with_memory_space_constraint(table_part, pltpu.HBM) for table_part in tables]
+    args.append(pltpu.with_memory_space_constraint(sources, space))
     if previous is not None:
         in_specs.append(partial)
-        if not final:
-            aliases = {len(args): 0}
-        args.append(previous)
+        args.append(pltpu.with_memory_space_constraint(previous, pltpu.HBM))
     if final:
-        out_spec = pl.BlockSpec((group_rows, members, length), lambda g: (g, 0, 0))
+        out_spec = pl.BlockSpec((group_rows, members, length), lambda b: (b, 0, 0))
         out_shape = jax.ShapeDtypeStruct((groups * group_rows, members, length), jnp.float32)
     else:
         out_spec = partial
-        out_shape = jax.ShapeDtypeStruct((groups, 2 * LANES, length), jnp.float32)
+        out_shape = pltpu.HBM((groups * 2 * LANES, length), jnp.float32)
     return pl.pallas_call(
         body,
         grid=(groups,),
         in_specs=in_specs,
         out_specs=out_spec,
         out_shape=out_shape,
-        scratch_shapes=[
-            pltpu.VMEM((depth, length), jnp.bfloat16),
-            pltpu.VMEM((depth, length), jnp.bfloat16),
-            pltpu.VMEM((depth, 2 * LANES), jnp.float32),
-        ],
-        input_output_aliases=aliases,
-        compiler_params=pltpu.CompilerParams(dimension_semantics=("arbitrary",)),
+        compiler_params=pltpu.CompilerParams(
+            dimension_semantics=("arbitrary",), vmem_limit_bytes=26 * 2**20
+        ),
         cost_estimate=pl.CostEstimate(
             flops=6 * groups * 256 * depth * length, bytes_accessed=12 * 10**6, transcendentals=0
         ),
@@ -304,36 +324,42 @@
         group_rows -= 1
     groups = rows // group_rows
 
-    column = lax.broadcasted_iota(jnp.int32, (latitudes, latitudes), 1)
-    select = (lat_order[:, None] == column).astype(jnp.bfloat16)
+    order = lat_order.reshape(-1, LANES)
     base = (me * slots).reshape(1).astype(jnp.int32)
 
     old = dense(coeffs_old)
     fresh_noise = dense(noise)
     parts = chunks_of(slots)
+    last = len(parts) - 1
+    starts = [sum(parts[:i]) for i in range(len(parts))]
+    depths = [count * round_up(2 * size, 8) for size in parts]
     new = None
+    pattern = None
     received = []
-    start = 0
-    waves = wavenumber_of_slot
-    for size in parts:
+    tables = []
+    for index, size in enumerate(parts):
         new, messages = spectral(
-            old, fresh_noise, legendre, amplitude, decay, wavenumber_of_slot, base, select, shape,
-            start, size, new, count, groups, group_rows,
-        )
-        if start == 0:
-            messages, waves = lax.optimization_barrier((messages, waves))
+            old, fresh_noise, legendre, amplitude, decay, wavenumber_of_slot, base, order, shape,
+            starts[index], size, new, count, groups, group_rows,
+        )
+        if index == 0:
+            messages, waves = lax.optimization_barrier((messages, wavenumber_of_slot))
+            fine, coarse = synthesis_tables(waves.reshape(count, slots), parts, LON)
+            tables = [
+                expand_tables(fine, coarse, sum(depths[:i]), depths[i], LON) for i in range(len(parts))
+            ]
+        if index == 2:
+            pattern = synthesis(
+                tables[0], received[0], None, False, groups, group_rows, members
+            )
+        if index == last and index:
+            messages, pattern, tables = lax.optimization_barrier((messages, pattern, tables))
         received.append(lax.all_to_all(messages, AXES, 0, 0, tiled=True))
-        start += size
-    fine, coarse = synthesis_tables(waves.reshape(count, slots), parts, LON)
-    pattern = None
-    start = 0
-    for index, size in enumerate(parts):
-        depth = count * round_up(2 * size, 8)
+    for index in range(1 if last >= 2 else 0, len(parts)):
         pattern = synthesis(
-            fine[:, start : start + depth], coarse[:, start : start + depth], received[index],
-            pattern, index == len(parts) - 1, groups, group_rows, members, LON,
-        )
-        start += depth
+            tables[index], received[index], pattern, index == last,
+            groups, group_rows, members,
+        )
     return (undense(new, shape), pattern)
 
 

time: 164 us -> 156 us (0.951)
  waiting for transfers between devices: 62.8 us -> 54.1 us
  other arithmetic: 9.99 us -> 5.95 us
  local copies, waits for them, and re-layouts: 4.68 us -> 6.99 us
    all_to_all x3, waiting for transfers between devices: 62.8 us -> 54.1 us  [local(): received.append(lax.all_to_all(messages, AXES, 0, 0, tiled=True))]
    pallas_call x0 -> x3, Pallas kernels: none -> 4 us  [expand_tables(): pl.pallas_call(table_kernel, grid=(depth // rows,), in_specs=[factor, fac...]
    pallas_call x3, Pallas kernels: 27.9 us -> 25 us  [synthesis(): pl.pallas_call(body, grid=(groups,), in_specs=in_specs, out_specs=out_spe...]
    unnamed x10 -> x16, local copies, waits for them, and re-layouts: 3.69 us -> 5.99 us
    another operation x2 -> x1, other arithmetic: 2.38 us -> 0.17 us  [synthesis_tables(): fine = jnp.stack([weight * jnp.cos(near), weight * jnp.sin(near)])]
    convert_element_type x1 -> x0, other arithmetic: 1.83 us -> none  [local(): select = (lat_order[:, None] == column).astype(jnp.bfloat16)]
  transfers between devices with their start and end apart: 3 -> 3, of which waited for: 2 -> 3; matrix products, arithmetic and copies ran while one was open for 6% -> 5% of each run, Pallas kernels for 31% -> 34%
where the time goes in v1:
time: 156 us; the launch traced here: 154 us
  Pallas kernels  69 us (44%)
  waiting for transfers between devices  54.1 us (35%)
  starting transfers between devices  17.1 us (11%)
  local copies, waits for them, and re-layouts  6.99 us (4%)
  other arithmetic  5.95 us (4%)
    all_to_all x3, waiting for transfers between devices, local(): received.append(lax.all_to_all(messages, AXES, 0, 0, tiled=True))  54.1 us
    pallas_call x3, Pallas kernels, spectral(): pl.pallas_call(body, grid=(slots // unit,), in_specs=in_specs, out_specs=...  40 us
    pallas_call x3, Pallas kernels, synthesis(): pl.pallas_call(body, grid=(groups,), in_specs=in_specs, out_specs=out_spe...  25 us
    all_to_all x3, starting transfers between devices, local(): received.append(lax.all_to_all(messages, AXES, 0, 0, tiled=True))  17.1 us
    unnamed x16, local copies, waits for them, and re-layouts  5.99 us
    cos x1, other arithmetic, synthesis_tables(): coarse = jnp.stack([jnp.cos(far), jnp.sin(far)])  5.72 us
    pallas_call x3, Pallas kernels, expand_tables(): pl.pallas_call(table_kernel, grid=(depth // rows,), in_specs=[factor, fac...  4 us
  transfers between devices with their start and end apart: 3, of which 3 were waited for; matrix products, arithmetic and copies ran while one was open for 5% of the time, Pallas kernels for 34%

profile of v1, /device:TPU:0, one launch (start us, length us, event | category | flops | bytes accessed | tf_op | source)
XLA Modules:
  0.0 154.1 jit_solution(1408255969881411892)
XLA Ops:
  0.6 9.4 %spectral.3 = (f32[30000,128]{1,0:T(8,128)}, f32[2048,128]{1,0:T(8,128)}) custom-call(s32[1]{0:T(128)} %bitcast.refs_0_, s32[640]{0:T(1024)} %refs_1_.5, f32[3]{0:T(128)} %refs_2_.5, f32[30000,128]{1,0:T(8,128)} %bitcast.22, bf16[30000,128]{1,0:T(8,128)(2,1)} %bitcast.25, f32[20,640,640]{2,1,0:T(8,128)} %refs_5_.5, f32[3,640]{1,0:T(4,128)} %refs_6_.5, ...), custom_call_target="tpu_custom_call" | custom-call | flops 2000000000 | bytes 14000000 | tf_op jit(solution)/shard_map/spectral/pallas_call | solution.py:167
  10.0 7.5 %all-to-all-start = ((f32[32,64,128]{2,1,0:T(8,128)}), f32[32,64,128]{2,1,0:T(8,128)}, u32[]{:S(2)}, u32[]{:S(2)}) async-start(f32[32,64,128]{2,1,0:T(8,128)} %bitcast.30), calls=%async_computation | async-start | bytes 2097152 | tf_op jit(solution)/shard_map/all_to_all | solution.py:357
  17.5 21.1 %spectral.4 = (f32[30000,128]{1,0:T(8,128)}, f32[6144,128]{1,0:T(8,128)}) custom-call(s32[1]{0:T(128)S(6)} %add.67.refs_0_, s32[640]{0:T(1024)} %refs_1_.5, f32[3]{0:T(128)} %refs_2_.5, f32[30000,128]{1,0:T(8,128)} %bitcast.23, bf16[30000,128]{1,0:T(8,128)(2,1)} %bitcast.26, f32[20,640,640]{2,1,0:T(8,128)} %refs_5_.5, ...), custom_call_target="tpu_custom_call", output_to_operand_aliasing={{0}: (8, {})} | custom-call | flops 6000000000 | bytes 42000000 | tf_op jit(solution)/shard_map/spectral/pallas_call | solution.py:167
  38.7 3.7 %all-to-all-done.refs_2_ = f32[32,64,128]{2,1,0:T(8,128)} async-done(((f32[32,64,128]{2,1,0:T(8,128)}), f32[32,64,128]{2,1,0:T(8,128)}, u32[]{:S(2)}, u32[]{:S(2)}) %all-to-all-start) | async-done | bytes 1048608 | tf_op jit(solution)/shard_map/all_to_all | solution.py:357
  42.4 0.0 copy-start.6
  42.4 4.8 %all-to-all-start.2 = ((f32[32,192,128]{2,1,0:T(8,128)}), f32[32,192,128]{2,1,0:T(8,128)}, u32[]{:S(2)}, u32[]{:S(2)}) async-start(f32[32,192,128]{2,1,0:T(8,128)} %bitcast.29), calls=%async_computation.2 | async-start | bytes 6291456 | tf_op jit(solution)/shard_map/all_to_all | solution.py:357
  47.3 0.0 copy-done.6
  47.3 0.1 reshape.578
  47.4 0.1 slice.13
  47.5 0.1 fusion.16
  47.5 0.1 broadcast_in_dim.22
  47.6 0.2 concatenate.20
  47.8 0.1 broadcast_in_dim.23
  47.9 0.1 concatenate.21
  48.1 0.1 broadcast_in_dim.24
  48.2 0.2 concatenate.22
  48.5 5.7 %fusion.7 = (f32[1,1280,128]{2,1,0:T(8,128)S(1)}, f32[1,1280,128]{2,1,0:T(8,128)S(1)}, f32[1,1280,128]{2,1,0:T(8,128)S(1)}, f32[1,1280,128]{2,1,0:T(8,128)S(1)}) fusion(s32[128]{0:T(128)S(1)} %multiply_remainder_fusion.1, s32[128]{0:T(128)S(1)} %broadcast_add_fusion, s32[1280]{0:T(1024)S(1)} %broadcast_maximum_fusion, pred[128]{0:T(512)(128)(4,1)S(1)} %compare_and_fusion, ...), kind=kLoop, calls=%fused_computation.12 | loop fusion | flops 3932160 | bytes 2644352 | tf_op jit(solution)/shard_map/cos | solution.py:309
  54.2 0.2 pad_maximum_fusion
  54.4 0.8 tables.3
  55.1 0.0 copy-start.2
  55.2 0.8 copy-done.2
  56.0 0.0 copy-start.3
  56.0 0.8 copy-done.3
  56.8 0.8 tables.5
  57.6 0.0 copy-start
  57.6 0.8 copy-done
  58.5 0.0 copy-start.1
  58.5 0.8 copy-done.1
  59.3 2.5 %tables.4 = (bf16[768,1280]{1,0:T(8,128)(2,1)S(1)}, bf16[768,1280]{1,0:T(8,128)(2,1)S(1)}) custom-call(f32[2,1280,128]{2,1,0:T(8,128)S(1)} %get-tuple-element.50.fine, f32[2,1280,128]{2,1,0:T(8,128)S(1)} %get-tuple-element.51.coarse), custom_call_target="tpu_custom_call" | custom-call | flops 1500000000 | bytes 3932160 | tf_op jit(solution)/shard_map/tables/pallas_call | solution.py:210
  61.8 0.0 copy-start.4
  61.8 1.3 copy-done.4
  63.1 0.0 copy-start.5
  63.1 1.3 copy-done.5
  64.4 9.4 %spectral.5 = (f32[30000,128]{1,0:T(8,128)}, f32[2048,128]{1,0:T(8,128)}) custom-call(s32[1]{0:T(128)S(6)} %add.66.refs_0_, s32[640]{0:T(1024)} %refs_1_.5, f32[3]{0:T(128)} %refs_2_.5, f32[30000,128]{1,0:T(8,128)} %bitcast.24, bf16[30000,128]{1,0:T(8,128)(2,1)} %bitcast.27, f32[20,640,640]{2,1,0:T(8,128)} %refs_5_.5, ...), custom_call_target="tpu_custom_call", output_to_operand_aliasing={{0}: (8, {})} | custom-call | flops 2000000000 | bytes 14000000 | tf_op jit(solution)/shard_map/spectral/pallas_call | solution.py:167
  73.8 6.3 %synthesis.3.refs_3_ = f32[1024,1280]{1,0:T(8,128)} custom-call(bf16[256,1280]{1,0:T(8,128)(2,1)} %copy-done.2, bf16[256,1280]{1,0:T(8,128)(2,1)} %copy-done.3, f32[32,64,128]{2,1,0:T(8,128)} %all-to-all-done.refs_2_), custom_call_target="tpu_custom_call" | custom-call | flops 2013265920 | bytes 12000000 | tf_op jit(solution)/shard_map/synthesis/pallas_call | solution.py:276
  80.1 36.9 %all-to-all-done.2.refs_2_ = f32[32,192,128]{2,1,0:T(8,128)} async-done(((f32[32,192,128]{2,1,0:T(8,128)}), f32[32,192,128]{2,1,0:T(8,128)}, u32[]{:S(2)}, u32[]{:S(2)}) %all-to-all-start.2) | async-done | bytes 3145760 | tf_op jit(solution)/shard_map/all_to_all | solution.py:357
  117.1 4.8 %all-to-all-start.1 = ((f32[32,64,128]{2,1,0:T(8,128)}), f32[32,64,128]{2,1,0:T(8,128)S(1)}, u32[]{:S(2)}, u32[]{:S(2)}) async-start(f32[32,64,128]{2,1,0:T(8,128)} %bitcast.16), calls=%async_computation.1 | async-start | bytes 2097152 | tf_op jit(solution)/shard_map/all_to_all | solution.py:357
  121.9 11.5 %synthesis.4.refs_3_ = f32[1024,1280]{1,0:T(8,128)} custom-call(bf16[768,1280]{1,0:T(8,128)(2,1)} %copy-done.4, bf16[768,1280]{1,0:T(8,128)(2,1)} %copy-done.5, f32[32,192,128]{2,1,0:T(8,128)} %all-to-all-done.2.refs_2_, f32[1024,1280]{1,0:T(8,128)} %synthesis.3.refs_3_), custom_call_target="tpu_custom_call" | custom-call | flops 6039797760 | bytes 12000000 | tf_op jit(solution)/shard_map/synthesis/pallas_call | solution.py:276
  133.4 13.5 %all-to-all-done.1.refs_2_ = f32[32,64,128]{2,1,0:T(8,128)S(1)} async-done(((f32[32,64,128]{2,1,0:T(8,128)}), f32[32,64,128]{2,1,0:T(8,128)S(1)}, u32[]{:S(2)}, u32[]{:S(2)}) %all-to-all-start.1) | async-done | bytes 1048608 | tf_op jit(solution)/shard_map/all_to_all | solution.py:357
  146.8 7.2 %synthesis.5 = f32[20,50,1280]{2,1,0:T(8,128)} custom-call(bf16[256,1280]{1,0:T(8,128)(2,1)} %copy-done, bf16[256,1280]{1,0:T(8,128)(2,1)} %copy-done.1, f32[32,64,128]{2,1,0:T(8,128)S(1)} %all-to-all-done.1.refs_2_, f32[1024,1280]{1,0:T(8,128)} %synthesis.4.refs_3_), custom_call_target="tpu_custom_call" | custom-call | flops 2013265920 | bytes 12000000 | tf_op jit(solution)/shard_map/synthesis/pallas_call | solution.py:276
  (12 shorter events, 0.1 us)
Async XLA Ops:
  10.0 32.4 %all-to-all-start = ((f32[32,64,128]{2,1,0:T(8,128)}), f32[32,64,128]{2,1,0:T(8,128)}, u32[]{:S(2)}, u32[]{:S(2)}) async-start(f32[32,64,128]{2,1,0:T(8,128)} %bitcast.30), calls=%async_computation | async-start | bytes 2097152 | tf_op jit(solution)/shard_map/all_to_all | solution.py:357
  42.4 4.9 %copy-start.6 = (s32[640]{0:T(1024)S(1)}, s32[640]{0:T(1024)}, u32[]{:S(2)}) copy-start(s32[640]{0:T(1024)} %refs_1_.5) | copy-start | bytes 7684
  42.4 74.6 %all-to-all-start.2 = ((f32[32,192,128]{2,1,0:T(8,128)}), f32[32,192,128]{2,1,0:T(8,128)}, u32[]{:S(2)}, u32[]{:S(2)}) async-start(f32[32,192,128]{2,1,0:T(8,128)} %bitcast.29), calls=%async_computation.2 | async-start | bytes 6291456 | tf_op jit(solution)/shard_map/all_to_all | solution.py:357
  55.1 0.8 copy-start.2
  56.0 0.8 copy-start.3
  57.6 0.9 copy-start
  58.5 0.9 copy-start.1
  61.8 1.3 copy-start.4
  63.1 1.3 copy-start.5
  117.1 29.8 %all-to-all-start.1 = ((f32[32,64,128]{2,1,0:T(8,128)}), f32[32,64,128]{2,1,0:T(8,128)S(1)}, u32[]{:S(2)}, u32[]{:S(2)}) async-start(f32[32,64,128]{2,1,0:T(8,128)} %bitcast.16), calls=%async_computation.1 | async-start | bytes 2097152 | tf_op jit(solution)/shard_map/all_to_all | solution.py:357

commit v2 on v1

--- a/solution.py
+++ b/solution.py
@@ -13,11 +13,9 @@
 
 
 def chunks_of(slots):
-    if slots % 4:
-        return (slots,)
-    if slots >= 16:
-        return (4, slots - 8, 4)
-    return (slots,)
+    if slots % 4 or slots < 16:
+        return ((0, slots),)
+    return ((slots - 4, 4), (0, slots - 8), (slots - 8, 4))
 
 
 def round_up(value, unit):
@@ -40,10 +38,12 @@
 
 
 def spectral_kernel(
-    first, slots, unit, count, groups, group_rows, members, rows_p, scales, width, base, waves,
+    fill, first, start, slots, unit, count, groups, group_rows, members, rows_p, scales, width, base, waves,
     decay, old, noise, legendre, amplitude, order, *rest
 ):
-    new, out, drive, loud, spectrum, rows, select = rest[0 if first else 1 :]
+    rest = rest[0 if first else 1 :]
+    new = rest[0] if fill else None
+    out, drive, loud, spectrum, rows, select, bases, sems = rest[1 if fill else 0 :]
     step = pl.program_id(0)
     half = spectrum.shape[1] // 4
     blocks = count * groups
@@ -73,67 +73,122 @@
     lane = lax.broadcasted_iota(jnp.int32, (1, LANES), 1)
     wide_lane = lax.broadcasted_iota(jnp.int32, (blocks, LANES), 1)
     nt = (((1,), (1,)), ((), ()))
-    for u in range(unit):
-        wave = waves[base[0] + step * unit + u]
-        gains = pltpu.roll(drive[...], lax.rem(width - wave, width), 1)
-        for tile in range(tiles):
-            live = lane + (tile * LANES) + wave < width
-            keep = [jnp.where(live, decay[k], 0.0) for k in range(scales)]
-            gain = [
-                jnp.where(live, gains[k : k + 1, tile * LANES : (tile + 1) * LANES], 0.0)
-                for k in range(scales)
-            ]
+    steps = slots // unit
+    levels = sorted({max(1, 2 * tiles // 5), tiles})
+    buffer = lax.rem(step, 2)
+
+    def is_level(index, level):
+        lowest = waves[base[0] + index * unit]
+        for u in range(1, unit):
+            lowest = jnp.minimum(lowest, waves[base[0] + index * unit + u])
+        few = lowest + levels[0] * LANES >= width
+        return few if level != tiles else jnp.logical_not(few)
+
+    def copies(index, level):
+        reach = pl.ds(0, level * LANES)
+        into = lax.rem(index, 2)
+        return [
+            pltpu.make_async_copy(
+                legendre.at[start + index * unit + u, :, reach],
+                bases.at[into, u, :, reach],
+                sems.at[into, u],
+            )
+            for u in range(unit)
+        ]
+
+    def begin_copies(index):
+        for level in levels:
+
+            @pl.when(is_level(index, level))
+            def _():
+                for copy in copies(index, level):
+                    copy.start()
+
+    @pl.when(step == 0)
+    def _():
+        begin_copies(0)
+
+    @pl.when(step + 1 < steps)
+    def _():
+        begin_copies(step + 1)
+
+    def work(level):
+        for copy in copies(step, level):
+            copy.wait()
+        for u in range(unit):
+            wave = waves[base[0] + step * unit + u]
+            gains = pltpu.roll(drive[...], lax.rem(width - wave, width), 1)
+            for tile in range(level if fill else tiles, tiles):
+                for r in range(2):
+                    for k in range(scales):
+                        at = pl.ds(u * per_slot + k * members * stride + 2 * tile + r, members, stride=stride)
+                        new[at, :] = jnp.zeros((members, LANES), jnp.float32)
+            for tile in range(level):
+                live = lane + (tile * LANES) + wave < width
+                keep = [jnp.where(live, decay[k], 0.0) for k in range(scales)]
+                gain = [
+                    jnp.where(live, gains[k : k + 1, tile * LANES : (tile + 1) * LANES], 0.0)
+                    for k in range(scales)
+                ]
+                for r in range(2):
+                    total = None
+                    for k in range(scales):
+                        at = pl.ds(u * per_slot + k * members * stride + 2 * tile + r, members, stride=stride)
+                        fresh = keep[k] * old[at, :] + gain[k] * loud[at, :]
+                        if fill:
+                            new[at, :] = fresh
+                        total = fresh if total is None else total + fresh
+                    high = total.astype(jnp.bfloat16)
+                    low = (total - high.astype(jnp.float32)).astype(jnp.bfloat16)
+                    cut = slice(tile * LANES, (tile + 1) * LANES)
+                    spectrum[u, r * half : r * half + members, cut] = high
+                    spectrum[u, (2 + r) * half : (2 + r) * half + members, cut] = low
+            reach = level * LANES
+            basis = bases[buffer, u, :, :reach]
+            basis_high = basis.astype(jnp.bfloat16)
+            basis_low = (basis - basis_high.astype(jnp.float32)).astype(jnp.bfloat16)
+            wide = lax.dot_general(basis_high, spectrum[u, :, :reach], nt, preferred_element_type=jnp.float32)
+            narrow = lax.dot_general(
+                basis_low, spectrum[u, : 2 * half, :reach], nt, preferred_element_type=jnp.float32
+            )
+            field = wide[:, : 2 * half] + wide[:, 2 * half :] + narrow
+            field_high = field.astype(jnp.bfloat16)
+            field_low = (field - field_high.astype(jnp.float32)).astype(jnp.bfloat16)
+            both = jnp.dot(
+                select[...],
+                jnp.concatenate([field_high, field_low], axis=1),
+                preferred_element_type=jnp.float32,
+            )
+            rows[u] = both[:, : 2 * half] + both[:, 2 * half :]
             for r in range(2):
-                total = None
-                for k in range(scales):
-                    at = pl.ds(u * per_slot + k * members * stride + 2 * tile + r, members, stride=stride)
-                    fresh = keep[k] * old[at, :] + gain[k] * loud[at, :]
-                    new[at, :] = fresh
-                    total = fresh if total is None else total + fresh
-                high = total.astype(jnp.bfloat16)
-                low = (total - high.astype(jnp.float32)).astype(jnp.bfloat16)
-                cut = slice(tile * LANES, (tile + 1) * LANES)
-                spectrum[u, r * half : r * half + members, cut] = high
-                spectrum[u, (2 + r) * half : (2 + r) * half + members, cut] = low
-        basis = legendre[u]
-        basis_high = basis.astype(jnp.bfloat16)
-        basis_low = (basis - basis_high.astype(jnp.float32)).astype(jnp.bfloat16)
-        wide = lax.dot_general(basis_high, spectrum[u], nt, preferred_element_type=jnp.float32)
-        narrow = lax.dot_general(
-            basis_low, spectrum[u, : 2 * half], nt, preferred_element_type=jnp.float32
-        )
-        field = wide[:, : 2 * half] + wide[:, 2 * half :] + narrow
-        field_high = field.astype(jnp.bfloat16)
-        field_low = (field - field_high.astype(jnp.float32)).astype(jnp.bfloat16)
-        both = jnp.dot(
-            select[...],
-            jnp.concatenate([field_high, field_low], axis=1),
-            preferred_element_type=jnp.float32,
-        )
-        rows[u] = both[:, : 2 * half] + both[:, 2 * half :]
-        for r in range(2):
-            packed = [None, None]
-            for i in range(group_rows):
-                start = i * members
-                piece = rows[u, pl.ds(i, blocks, stride=group_rows), :]
-                shift = (start - r * half) % LANES
-                if shift:
-                    piece = pltpu.roll(piece, shift, 1)
+                packed = [None, None]
+                for i in range(group_rows):
+                    start = i * members
+                    piece = rows[u, pl.ds(i, blocks, stride=group_rows), :]
+                    shift = (start - r * half) % LANES
+                    if shift:
+                        piece = pltpu.roll(piece, shift, 1)
+                    for tile in range(2):
+                        begin = max(start - tile * LANES, 0)
+                        end = min(start + members - tile * LANES, LANES)
+                        if begin >= end:
+                            continue
+                        if packed[tile] is None:
+                            packed[tile] = piece
+                        else:
+                            packed[tile] = jnp.where(wide_lane < begin, packed[tile], piece)
                 for tile in range(2):
-                    begin = max(start - tile * LANES, 0)
-                    end = min(start + members - tile * LANES, LANES)
-                    if begin >= end:
-                        continue
-                    if packed[tile] is None:
-                        packed[tile] = piece
-                    else:
-                        packed[tile] = jnp.where(wide_lane < begin, packed[tile], piece)
-            for tile in range(2):
-                at = pl.ds(tile * rows_p + 2 * (step * unit + u) + r, blocks, stride=2 * rows_p)
-                out[at, :] = packed[tile]
-
-
-def spectral(old, noise, legendre, amplitude, decay, waves, base, order, shape, start, slots, previous, count, groups, group_rows):
+                    at = pl.ds(tile * rows_p + 2 * (step * unit + u) + r, blocks, stride=2 * rows_p)
+                    out[at, :] = packed[tile]
+
+    for level in levels:
+
+        @pl.when(is_level(step, level))
+        def _():
+            work(level)
+
+
+def spectral(old, noise, legendre, amplitude, decay, waves, base, order, shape, start, slots, fill, previous, count, groups, group_rows):
     _, _, scales, members, width = shape
     unit = 2 if slots % 2 == 0 else slots
     rows_p = round_up(2 * slots, 8)
@@ -144,7 +199,7 @@
 
     def body(*refs):
         spectral_kernel(
-            first, slots, unit, count, groups, group_rows, members, rows_p, scales, width, *refs
+            fill, first, start, slots, unit, count, groups, group_rows, members, rows_p, scales, width, *refs
         )
 
     state = pl.BlockSpec((block, LANES), lambda i: (skip + i, 0))
@@ -154,7 +209,7 @@
         pl.BlockSpec(memory_space=pltpu.SMEM),
         state,
         state,
-        pl.BlockSpec((unit,) + legendre.shape[1:], lambda i: (skip + i, 0, 0)),
+        pl.BlockSpec(memory_space=pl.ANY),
         pl.BlockSpec(amplitude.shape, lambda i: (0, 0)),
         pl.BlockSpec(order.shape, lambda i: (0, 0)),
     ]
@@ -164,21 +219,21 @@
         in_specs.append(pl.BlockSpec(memory_space=pl.ANY))
         aliases = {len(args): 0}
         args.append(previous)
-    new, messages = pl.pallas_call(
+    results = pl.pallas_call(
         body,
         grid=(slots // unit,),
         in_specs=in_specs,
-        out_specs=[state, pl.BlockSpec((count * size, LANES), lambda i: (0, 0))],
-        out_shape=[
-            jax.ShapeDtypeStruct(old.shape, jnp.float32),
-            jax.ShapeDtypeStruct((count * size, LANES), jnp.float32),
-        ],
+        out_specs=[state] * fill + [pl.BlockSpec((count * size, LANES), lambda i: (0, 0))],
+        out_shape=[jax.ShapeDtypeStruct(old.shape, jnp.float32)] * fill
+        + [jax.ShapeDtypeStruct((count * size, LANES), jnp.float32)],
         scratch_shapes=[
             pltpu.VMEM((8, width), jnp.float32),
             pltpu.VMEM((block, LANES), jnp.float32),
             pltpu.VMEM((unit, 4 * 64, width), jnp.bfloat16),
             pltpu.VMEM((unit, legendre.shape[1], LANES), jnp.float32),
             pltpu.VMEM((legendre.shape[1], legendre.shape[1]), jnp.bfloat16),
+            pltpu.VMEM((2, unit) + legendre.shape[1:], jnp.float32),
+            pltpu.SemaphoreType.DMA((2, unit)),
         ],
         input_output_aliases=aliases,
         compiler_params=pltpu.CompilerParams(
@@ -189,7 +244,68 @@
         ),
         name="spectral",
     )(*args)
-    return new, messages.reshape(count, size, LANES)
+    return results[0] if fill else None, results[-1].reshape(count, size, LANES)
+
+
+def update_kernel(start, unit, members, scales, width, base, waves, decay, old, noise, amplitude, _, new, drive, loud):
+    tiles = width // LANES
+    stride = 2 * tiles
+    for k in range(scales):
+        d = jnp.full((1, LANES), decay[k], jnp.float32)
+        drive[k : k + 1] = amplitude[k : k + 1] * jnp.sqrt(1.0 - d * d)[:, :1]
+    loud[...] = noise[...].astype(jnp.float32)
+    lane = lax.broadcasted_iota(jnp.int32, (1, LANES), 1)
+    for u in range(unit):
+        wave = waves[base[0] + pl.program_id(0) * unit + u]
+        gains = pltpu.roll(drive[...], lax.rem(width - wave, width), 1)
+        for tile in range(tiles):
+            live = lane + (tile * LANES) + wave < width
+            for k in range(scales):
+                keep = jnp.where(live, decay[k], 0.0)
+                gain = jnp.where(live, gains[k : k + 1, tile * LANES : (tile + 1) * LANES], 0.0)
+                for r in range(2):
+                    row = (u * scales + k) * members * stride + 2 * tile + r
+                    at = pl.ds(row, members, stride=stride)
+                    new[at, :] = keep * old[at, :] + gain * loud[at, :]
+
+
+def update(old, noise, amplitude, decay, waves, base, shape, start, slots, previous):
+    _, _, scales, members, width = shape
+    unit = 2
+    block = unit * scales * members * 2 * (width // LANES)
+    skip = start // unit
+
+    def body(*refs):
+        update_kernel(start, unit, members, scales, width, *refs)
+
+    state = pl.BlockSpec((block, LANES), lambda i: (skip + i, 0))
+    return pl.pallas_call(
+        body,
+        grid=(slots // unit,),
+        in_specs=[
+            pl.BlockSpec(memory_space=pltpu.SMEM),
+            pl.BlockSpec(memory_space=pltpu.SMEM),
+            pl.BlockSpec(memory_space=pltpu.SMEM),
+            state,
+            state,
+            pl.BlockSpec(amplitude.shape, lambda i: (0, 0)),
+            pl.BlockSpec(memory_space=pl.ANY),
+        ],
+        out_specs=state,
+        out_shape=jax.ShapeDtypeStruct(old.shape, jnp.float32),
+        scratch_shapes=[
+            pltpu.VMEM((8, width), jnp.float32),
+            pltpu.VMEM((block, LANES), jnp.float32),
+        ],
+        input_output_aliases={6: 0},
+        compiler_params=pltpu.CompilerParams(
+            dimension_semantics=("arbitrary",), vmem_limit_bytes=65400 * 2**10
+        ),
+        cost_estimate=pl.CostEstimate(
+            flops=slots * 10**8, bytes_accessed=slots * 1900000, transcendentals=0
+        ),
+        name="update",
+    )(base + start, waves, decay, old, noise, amplitude, previous)
 
 
 def table_kernel(fine, coarse, high, low):
@@ -261,8 +377,8 @@
     table = pl.BlockSpec((depth, length), lambda b: (0, 0))
     partial = pl.BlockSpec((2 * LANES, length), lambda b: (b, 0))
     in_specs = [table, table, pl.BlockSpec((sources.shape[0], 2 * rows_p, LANES), lambda b: (0, b, 0))]
-    space = pltpu.VMEM if final else pltpu.HBM
-    args = [pltpu.with_memory_space_constraint(table_part, pltpu.HBM) for table_part in tables]
+    space = pltpu.VMEM if final and sources.size < 2**19 else pltpu.HBM
+    args = [pltpu.with_memory_space_constraint(part, space) for part in tables]
     args.append(pltpu.with_memory_space_constraint(sources, space))
     if previous is not None:
         in_specs.append(partial)
@@ -292,12 +408,10 @@
 def synthesis_tables(waves, parts, length):
     count, slots = waves.shape
     numbers = []
-    start = 0
-    for size in parts:
+    for start, size in parts:
         rows = jnp.repeat(waves[:, start : start + size], 2, axis=1)
         pad = round_up(2 * size, 8) - 2 * size
         numbers.append(jnp.pad(rows, ((0, 0), (0, pad)), constant_values=-1).reshape(-1))
-        start += size
     number = jnp.concatenate(numbers)[:, None]
     lane = lax.broadcasted_iota(jnp.int32, (number.shape[0], LANES), 1)
     part = lax.broadcasted_iota(jnp.int32, (number.shape[0], LANES), 0) % 2
@@ -331,16 +445,15 @@
     fresh_noise = dense(noise)
     parts = chunks_of(slots)
     last = len(parts) - 1
-    starts = [sum(parts[:i]) for i in range(len(parts))]
-    depths = [count * round_up(2 * size, 8) for size in parts]
+    depths = [count * round_up(2 * size, 8) for _, size in parts]
     new = None
     pattern = None
     received = []
     tables = []
-    for index, size in enumerate(parts):
+    for index, (start, size) in enumerate(parts):
         new, messages = spectral(
             old, fresh_noise, legendre, amplitude, decay, wavenumber_of_slot, base, order, shape,
-            starts[index], size, new, count, groups, group_rows,
+            start, size, index > 0 or last == 0, new, count, groups, group_rows,
         )
         if index == 0:
             messages, waves = lax.optimization_barrier((messages, wavenumber_of_slot))
@@ -353,7 +466,12 @@
                 tables[0], received[0], None, False, groups, group_rows, members
             )
         if index == last and index:
-            messages, pattern, tables = lax.optimization_barrier((messages, pattern, tables))
+            new = update(
+                old, fresh_noise, amplitude, decay, wavenumber_of_slot, base, shape, *parts[0], new
+            )
+            messages, pattern, tables, new = lax.optimization_barrier(
+                (messages, pattern, tables, new)
+            )
         received.append(lax.all_to_all(messages, AXES, 0, 0, tiled=True))
     for index in range(1 if last >= 2 else 0, len(parts)):
         pattern = synthesis(

time: 156 us -> 154 us (0.987)
  waiting for transfers between devices: 54.1 us -> 51.2 us
  Pallas kernels: 69 us -> 71.4 us
  local copies, waits for them, and re-layouts: 6.99 us -> 5.2 us
    pallas_call x0 -> x1, Pallas kernels: none -> 3.83 us  [update(): pl.pallas_call(body, grid=(slots // unit,), in_specs=[pl.BlockSpec(memory...]
    all_to_all x3, waiting for transfers between devices: 54.1 us -> 51.2 us  [local(): received.append(lax.all_to_all(messages, AXES, 0, 0, tiled=True))]
    unnamed x16 -> x12, local copies, waits for them, and re-layouts: 5.99 us -> 4.27 us
  transfers between devices with their start and end apart: 3 -> 3, of which waited for: 3 -> 3; matrix products, arithmetic and copies ran while one was open for 5% -> 5% of each run, Pallas kernels for 34% -> 38%
where the time goes in v2:
time: 154 us; the launch traced here: 152 us
  Pallas kernels  71.4 us (46%)
  waiting for transfers between devices  51.2 us (33%)
  starting transfers between devices  17.2 us (11%)
  other arithmetic  5.95 us (4%)
  local copies, waits for them, and re-layouts  5.2 us (3%)
    all_to_all x3, waiting for transfers between devices, local(): received.append(lax.all_to_all(messages, AXES, 0, 0, tiled=True))  51.2 us
    pallas_call x3, Pallas kernels, spectral(): pl.pallas_call(body, grid=(slots // unit,), in_specs=in_specs, out_specs=...  39.2 us
    pallas_call x3, Pallas kernels, synthesis(): pl.pallas_call(body, grid=(groups,), in_specs=in_specs, out_specs=out_spe...  24.4 us
    all_to_all x3, starting transfers between devices, local(): received.append(lax.all_to_all(messages, AXES, 0, 0, tiled=True))  17.2 us
    cos x1, other arithmetic, synthesis_tables(): coarse = jnp.stack([jnp.cos(far), jnp.sin(far)])  5.72 us
    unnamed x12, local copies, waits for them, and re-layouts  4.27 us
    pallas_call x3, Pallas kernels, expand_tables(): pl.pallas_call(table_kernel, grid=(depth // rows,), in_specs=[factor, fac...  4.01 us
    pallas_call x1, Pallas kernels, update(): pl.pallas_call(body, grid=(slots // unit,), in_specs=[pl.BlockSpec(memory...  3.83 us
  transfers between devices with their start and end apart: 3, of which 3 were waited for; matrix products, arithmetic and copies ran while one was open for 5% of the time, Pallas kernels for 38%

profile of v2, /device:TPU:0, one launch (start us, length us, event | category | flops | bytes accessed | tf_op | source)
XLA Modules:
  0.0 151.8 jit_solution(16338282577351444609)
XLA Ops:
  0.6 7.5 %spectral.5 = f32[2048,128]{1,0:T(8,128)} custom-call(s32[1]{0:T(128)S(6)} %add.68.refs_0_, s32[640]{0:T(1024)} %refs_1_.7, f32[3]{0:T(128)} %refs_2_.7, f32[30000,128]{1,0:T(8,128)} %bitcast.23, bf16[30000,128]{1,0:T(8,128)(2,1)} %bitcast.27, f32[20,640,640]{2,1,0:T(8,128)} %refs_5_.6, f32[3,640]{1,0:T(4,128)} %refs_5_.7, s32[5,128]{1,0:T(8,128)} %bitcast.35), custom_call_target="tpu_custom_call" | custom-call | flops 2000000000 | bytes 14000000 | tf_op jit(solution)/shard_map/spectral/pallas_call | solution.py:222
  8.1 7.5 %all-to-all-start = ((f32[32,64,128]{2,1,0:T(8,128)}), f32[32,64,128]{2,1,0:T(8,128)}, u32[]{:S(2)}, u32[]{:S(2)}) async-start(f32[32,64,128]{2,1,0:T(8,128)} %bitcast.32), calls=%async_computation | async-start | bytes 2097152 | tf_op jit(solution)/shard_map/all_to_all | solution.py:475
  15.6 23.5 %spectral.3 = (f32[30000,128]{1,0:T(8,128)}, f32[6144,128]{1,0:T(8,128)}) custom-call(s32[1]{0:T(128)} %bitcast.refs_0_, s32[640]{0:T(1024)} %refs_1_.7, f32[3]{0:T(128)} %refs_2_.7, f32[30000,128]{1,0:T(8,128)} %bitcast.24, bf16[30000,128]{1,0:T(8,128)(2,1)} %bitcast.28, f32[20,640,640]{2,1,0:T(8,128)} %refs_5_.6, f32[3,640]{1,0:T(4,128)} %refs_5_.7, ...), custom_call_target="tpu_custom_call" | custom-call | flops 6000000000 | bytes 42000000 | tf_op jit(solution)/shard_map/spectral/pallas_call | solution.py:222
  39.1 1.4 all-to-all-done.refs_2_
  40.5 0.0 copy-start.4
  40.5 4.8 %all-to-all-start.2 = ((f32[32,192,128]{2,1,0:T(8,128)}), f32[32,192,128]{2,1,0:T(8,128)}, u32[]{:S(2)}, u32[]{:S(2)}) async-start(f32[32,192,128]{2,1,0:T(8,128)} %bitcast.33), calls=%async_computation.2 | async-start | bytes 6291456 | tf_op jit(solution)/shard_map/all_to_all | solution.py:475
  45.4 0.0 copy-done.4
  45.4 0.1 reshape.576
  45.5 0.1 fusion.16
  45.6 0.1 broadcast_in_dim.22
  45.7 0.2 concatenate.20
  45.8 0.1 broadcast_in_dim.23
  46.0 0.1 concatenate.21
  46.1 0.1 broadcast_in_dim.24
  46.2 0.2 concatenate.22
  46.4 8.2 %spectral.4 = (f32[30000,128]{1,0:T(8,128)}, f32[2048,128]{1,0:T(8,128)}) custom-call(s32[1]{0:T(128)S(6)} %add.67.refs_0_, s32[640]{0:T(1024)} %refs_1_.7, f32[3]{0:T(128)} %refs_2_.7, f32[30000,128]{1,0:T(8,128)} %bitcast.25, bf16[30000,128]{1,0:T(8,128)(2,1)} %bitcast.29, f32[20,640,640]{2,1,0:T(8,128)} %refs_5_.6, ...), custom_call_target="tpu_custom_call", output_to_operand_aliasing={{0}: (8, {})} | custom-call | flops 2000000000 | bytes 14000000 | tf_op jit(solution)/shard_map/spectral/pallas_call | solution.py:222
  54.5 3.8 %update.1 = f32[30000,128]{1,0:T(8,128)} custom-call(s32[1]{0:T(128)S(6)} %add.68.refs_0_, s32[640]{0:T(1024)} %refs_1_.7, f32[3]{0:T(128)} %refs_2_.7, f32[30000,128]{1,0:T(8,128)} %bitcast.26, bf16[30000,128]{1,0:T(8,128)(2,1)} %bitcast.30, f32[3,640]{1,0:T(4,128)} %refs_5_.7, f32[30000,128]{1,0:T(8,128)} %get-tuple-element.31.refs_6_), custom_call_target="tpu_custom_call", output_to_operand_aliasing={{}: (6, {})} | custom-call | flops 400000000 | bytes 7600000 | tf_op jit(solution)/shard_map/update/pallas_call | solution.py:282
  58.5 5.7 %fusion.7 = (f32[1,1280,128]{2,1,0:T(8,128)S(1)}, f32[1,1280,128]{2,1,0:T(8,128)S(1)}, f32[1,1280,128]{2,1,0:T(8,128)S(1)}, f32[1,1280,128]{2,1,0:T(8,128)S(1)}) fusion(s32[128]{0:T(128)S(1)} %multiply_remainder_fusion.1, s32[128]{0:T(128)S(1)} %broadcast_add_fusion, s32[1280]{0:T(1024)S(1)} %broadcast_maximum_fusion, pred[128]{0:T(512)(128)(4,1)S(1)} %compare_and_fusion, ...), kind=kLoop, calls=%fused_computation.12 | loop fusion | flops 3932160 | bytes 2644352 | tf_op jit(solution)/shard_map/cos | solution.py:423
  64.2 0.2 pad_maximum_fusion
  64.4 0.8 tables.3
  65.2 0.0 copy-start
  65.2 0.8 copy-done
  66.0 0.0 copy-start.1
  66.0 0.8 copy-done.1
  66.9 0.8 tables.5
  67.7 2.5 %tables.4 = (bf16[768,1280]{1,0:T(8,128)(2,1)S(1)}, bf16[768,1280]{1,0:T(8,128)(2,1)S(1)}) custom-call(f32[2,1280,128]{2,1,0:T(8,128)S(1)} %get-tuple-element.48.fine, f32[2,1280,128]{2,1,0:T(8,128)S(1)} %get-tuple-element.49.coarse), custom_call_target="tpu_custom_call" | custom-call | flops 1500000000 | bytes 3932160 | tf_op jit(solution)/shard_map/tables/pallas_call | solution.py:326
  70.1 0.0 copy-start.2
  70.1 1.3 copy-done.2
  71.5 0.0 copy-start.3
  71.5 1.3 copy-done.3
  72.7 6.1 %synthesis.3.refs_3_ = f32[1024,1280]{1,0:T(8,128)} custom-call(bf16[256,1280]{1,0:T(8,128)(2,1)} %copy-done, bf16[256,1280]{1,0:T(8,128)(2,1)} %copy-done.1, f32[32,64,128]{2,1,0:T(8,128)} %all-to-all-done.refs_2_), custom_call_target="tpu_custom_call" | custom-call | flops 2013265920 | bytes 12000000 | tf_op jit(solution)/shard_map/synthesis/pallas_call | solution.py:392
  78.8 36.4 %all-to-all-done.2.refs_2_ = f32[32,192,128]{2,1,0:T(8,128)} async-done(((f32[32,192,128]{2,1,0:T(8,128)}), f32[32,192,128]{2,1,0:T(8,128)}, u32[]{:S(2)}, u32[]{:S(2)}) %all-to-all-start.2) | async-done | bytes 3145760 | tf_op jit(solution)/shard_map/all_to_all | solution.py:475
  115.2 4.8 %all-to-all-start.1 = ((f32[32,64,128]{2,1,0:T(8,128)}), f32[32,64,128]{2,1,0:T(8,128)S(1)}, u32[]{:S(2)}, u32[]{:S(2)}) async-start(f32[32,64,128]{2,1,0:T(8,128)} %bitcast.12), calls=%async_computation.1 | async-start | bytes 2097152 | tf_op jit(solution)/shard_map/all_to_all | solution.py:475
  120.0 11.5 %synthesis.4.refs_3_ = f32[1024,1280]{1,0:T(8,128)} custom-call(bf16[768,1280]{1,0:T(8,128)(2,1)} %copy-done.2, bf16[768,1280]{1,0:T(8,128)(2,1)} %copy-done.3, f32[32,192,128]{2,1,0:T(8,128)} %all-to-all-done.2.refs_2_, f32[1024,1280]{1,0:T(8,128)} %synthesis.3.refs_3_), custom_call_target="tpu_custom_call" | custom-call | flops 6039797760 | bytes 12000000 | tf_op jit(solution)/shard_map/synthesis/pallas_call | solution.py:392
  131.5 13.4 %all-to-all-done.1.refs_2_ = f32[32,64,128]{2,1,0:T(8,128)S(1)} async-done(((f32[32,64,128]{2,1,0:T(8,128)}), f32[32,64,128]{2,1,0:T(8,128)S(1)}, u32[]{:S(2)}, u32[]{:S(2)}) %all-to-all-start.1) | async-done | bytes 1048608 | tf_op jit(solution)/shard_map/all_to_all | solution.py:475
  145.0 6.8 %synthesis.5 = f32[20,50,1280]{2,1,0:T(8,128)} custom-call(bf16[256,1280]{1,0:T(8,128)(2,1)S(1)} %get-tuple-element.33.refs_0_, bf16[256,1280]{1,0:T(8,128)(2,1)S(1)} %get-tuple-element.34.refs_1_, f32[32,64,128]{2,1,0:T(8,128)S(1)} %all-to-all-done.1.refs_2_, f32[1024,1280]{1,0:T(8,128)} %synthesis.4.refs_3_), custom_call_target="tpu_custom_call" | custom-call | flops 2013265920 | bytes 12000000 | tf_op jit(solution)/shard_map/synthesis/pallas_call | solution.py:392
  (12 shorter events, 0.1 us)
Async XLA Ops:
  8.1 32.4 %all-to-all-start = ((f32[32,64,128]{2,1,0:T(8,128)}), f32[32,64,128]{2,1,0:T(8,128)}, u32[]{:S(2)}, u32[]{:S(2)}) async-start(f32[32,64,128]{2,1,0:T(8,128)} %bitcast.32), calls=%async_computation | async-start | bytes 2097152 | tf_op jit(solution)/shard_map/all_to_all | solution.py:475
  40.5 4.9 %copy-start.4 = (s32[640]{0:T(1024)S(1)}, s32[640]{0:T(1024)}, u32[]{:S(2)}) copy-start(s32[640]{0:T(1024)} %refs_1_.7) | copy-start | bytes 7684
  40.5 74.6 %all-to-all-start.2 = ((f32[32,192,128]{2,1,0:T(8,128)}), f32[32,192,128]{2,1,0:T(8,128)}, u32[]{:S(2)}, u32[]{:S(2)}) async-start(f32[32,192,128]{2,1,0:T(8,128)} %bitcast.33), calls=%async_computation.2 | async-start | bytes 6291456 | tf_op jit(solution)/shard_map/all_to_all | solution.py:475
  65.2 0.8 copy-start
  66.0 0.9 copy-start.1
  70.1 1.3 copy-start.2
  71.5 1.3 copy-start.3
  115.2 29.8 %all-to-all-start.1 = ((f32[32,64,128]{2,1,0:T(8,128)}), f32[32,64,128]{2,1,0:T(8,128)S(1)}, u32[]{:S(2)}, u32[]{:S(2)}) async-start(f32[32,64,128]{2,1,0:T(8,128)} %bitcast.12), calls=%async_computation.1 | async-start | bytes 2097152 | tf_op jit(solution)/shard_map/all_to_all | solution.py:475
